TPU v7x, 32 devices: a whole 2x2x4 slice. The times are simulated.
32 devices in a mesh: pts: 8 (over y, x, core), wid: 4 (over z).
Axes of the slice: x: 2, y: 2, z: 4, core: 2. Of those that a mesh axis runs over, the one named last changes fastest.
Arguments:
- vertex_features: bfloat16 [90112, 512], P('pts'), may hold values from -40 to 40, as said below
- entry_matrix: bfloat16 [512, 512], P(None, 'wid'), may hold values from -2 to 2, as said below
- partition_matrix: bfloat16 [64, 32], replicated, may hold values from -3 to 3, as said below
- sharpness_matrix: float32 [64], replicated, may hold values from -3 to 3, as said below
- summary_qkv_matrix: float32 [3, 64, 64], replicated, may hold values from -3 to 3
- exit_matrix: bfloat16 [512, 512], P('wid'), may hold values from -0.5 to 0.5
- widening_matrix: bfloat16 [512, 512], P('wid'), may hold values from -0.25 to 0.25
- narrowing_matrix: bfloat16 [512, 512], P('wid'), may hold values from -0.25 to 0.25
Outputs:
- result: bfloat16 [90112, 512], P(('pts', 'wid'))
Inputs may be any that keep to these rules, and one draw needn't show every extreme that they name: `vertex_features`: features of the points, of order one to ten. `entry_matrix`: weights of the point projection. `partition_matrix`: slice logit weights. `sharpness_matrix`: temperature weights.
All inputs are finite; a program needn't handle non-finite values.
Results may differ from a plain program's by a relative error of at most 0.013.
Values may be sent and summed in bfloat16 or wider, within the bound.
A program may use at most 128 MiB of HBM per device.

v0:
```python
import jax
import jax.numpy as jnp
from jax import lax
from jax.sharding import PartitionSpec as P


def layer_norm(values):
    centred = values - jnp.mean(values, axis=-1, keepdims=True)
    variance = jnp.mean(centred * centred, axis=-1, keepdims=True)
    return centred * lax.rsqrt(variance + 1e-05)


def project_tokens(token_rows, summary_qkv_matrix):
    highest = lax.Precision.HIGHEST
    queries = jnp.einsum("hgd,de->hge", token_rows, summary_qkv_matrix[0], precision=highest)
    keys_all = jnp.einsum("hgd,de->hge", token_rows, summary_qkv_matrix[1], precision=highest)
    value_rows_total = jnp.einsum(
        "hgd,de->hge", token_rows, summary_qkv_matrix[2], precision=highest
    )
    return (queries, keys_all, value_rows_total)


def local(
    vertex_features,
    entry_matrix,
    partition_matrix,
    sharpness_matrix,
    summary_qkv_matrix,
    exit_matrix,
    widening_matrix,
    narrowing_matrix,
):
    head_size = summary_qkv_matrix.shape[1]
    point_rows = vertex_features.shape[0]
    wid_count = lax.axis_size("wid")
    row_block = point_rows // wid_count
    features = vertex_features.astype(jnp.float32)
    normed = layer_norm(features).astype(jnp.bfloat16)
    feats = jnp.dot(normed, entry_matrix, preferred_element_type=jnp.float32).astype(jnp.bfloat16)
    local_heads = feats.shape[1] // head_size
    attention_cluster = feats.reshape(point_rows, local_heads, head_size)
    partition_sharpness = 0.5 + jax.nn.softplus(
        jnp.einsum(
            "kgv,v->kg", attention_cluster, sharpness_matrix, preferred_element_type=jnp.float32
        )
    )
    partition_scores = jnp.einsum(
        "nhd,dg->nhg", attention_cluster, partition_matrix, preferred_element_type=jnp.float32
    )
    partition_mapping = jax.nn.softmax(
        partition_scores / partition_sharpness[:, :, None], axis=-1
    ).astype(jnp.bfloat16)
    numerator = jnp.einsum(
        "nhg,nhd->hgd", partition_mapping, attention_cluster, preferred_element_type=jnp.float32
    )
    mass = jnp.sum(partition_mapping, axis=0, dtype=jnp.float32)
    numerator, mass = lax.psum((numerator, mass), "pts")
    token_rows = numerator / (mass[:, :, None] + 1e-05)
    queries, keys_all, value_rows_total = project_tokens(token_rows, summary_qkv_matrix)
    highest = lax.Precision.HIGHEST
    scores = jnp.einsum("hge,hke->hgk", queries, keys_all, precision=highest) / jnp.sqrt(
        jnp.float32(head_size)
    )
    attend = jax.nn.softmax(scores, axis=-1)
    out_tok = jnp.einsum("hgk,hke->hge", attend, value_rows_total, precision=highest).astype(
        jnp.bfloat16
    )
    deslice = jnp.einsum(
        "nhg,hgd->nhd", partition_mapping, out_tok, preferred_element_type=jnp.float32
    ).astype(jnp.bfloat16)
    deslice = deslice.reshape(point_rows, local_heads * head_size)
    mixed_rows = lax.all_to_all(deslice, "wid", split_axis=0, concat_axis=1, tiled=True)
    out_full, up_full, down_full = (
        lax.all_gather(exit_matrix, "wid", axis=0, tiled=True),
        lax.all_gather(widening_matrix, "wid", axis=0, tiled=True),
        lax.all_gather(narrowing_matrix, "wid", axis=0, tiled=True),
    )
    attn_rows = jnp.dot(mixed_rows, out_full, preferred_element_type=jnp.float32)
    own_rows = lax.dynamic_slice_in_dim(features, lax.axis_index("wid") * row_block, row_block, 0)
    midway = own_rows + attn_rows
    normed2 = layer_norm(midway).astype(jnp.bfloat16)
    hidden = jax.nn.gelu(jnp.dot(normed2, up_full, preferred_element_type=jnp.float32)).astype(
        jnp.bfloat16
    )
    return (midway + jnp.dot(hidden, down_full, preferred_element_type=jnp.float32)).astype(
        jnp.bfloat16
    )


def solution(mesh):
    placed = (
        P("pts", None),
        P(None, "wid"),
        P(),
        P(),
        P(),
        P("wid", None),
        P("wid", None),
        P("wid", None),
    )
    return jax.shard_map(
        local, mesh=mesh, in_specs=placed, out_specs=P(("pts", "wid"), None), check_vma=False
    )
```

profile of v0, /device:TPU:0, one launch (start us, length us, event | category | flops | bytes accessed | tf_op | source)
XLA Modules:
  0.0 224.7 jit_solution(1888954604760041601)
XLA Ops:
  0.0 0.0 copy-start
  0.0 14.9 %copy.12 = bf16[11264,512]{0,1:T(8,128)(2,1)} copy(bf16[11264,512]{1,0:T(8,128)(2,1)} %param.8) | data formatting | bytes 23068672 | tf_op args[0]
  14.9 7.2 %convert_reduce_fusion = f32[11264]{0:T(1024)S(1)} fusion(bf16[11264,512]{0,1:T(8,128)(2,1)} %copy.12), kind=kLoop, calls=%fused_computation.3 | loop fusion | flops 11523072 | bytes 11579392 | tf_op jit(solution)/shard_map/reduce_sum | solution.py:8
  22.0 7.4 %multiply_reduce_fusion = f32[11264]{0:T(1024)S(1)} fusion(bf16[11264,512]{0,1:T(8,128)(2,1)} %copy.12, f32[11264]{0:T(1024)S(1)} %broadcast_multiply_fusion), kind=kLoop, calls=%fused_computation.2 | loop fusion | flops 23057408 | bytes 11624448 | tf_op jit(solution)/shard_map/reduce_sum | solution.py:9
  29.5 0.0 copy-done
  29.5 0.0 copy-start.6
  29.5 8.1 %convolution_convert_fusion.1 = bf16[11264,128]{0,1:T(8,128)(2,1)S(1)} fusion(bf16[512,128]{1,0:T(8,128)(2,1)S(1)} %copy-done, bf16[11264,512]{0,1:T(8,128)(2,1)} %copy.12, f32[11264]{0:T(1024)S(1)} %add_rsqrt_fusion, f32[11264]{0:T(1024)S(1)} %broadcast_multiply_fusion), kind=kOutput, calls=%fused_computation.5 | convolution fusion | flops 1500905472 | bytes 14639104 | tf_op jit(solution)/shard_map/dot_general | solution.py:39
  37.6 0.0 copy-start.3
  37.6 0.0 copy-done.6
  37.6 5.4 %fusion.48 = f32[1,11264,2]{0,1,2:T(8,128)} fusion(bf16[11264,2,64]{0,2,1:T(8,128)(2,1)S(1)} %bitcast.68, f32[64]{0:T(128)S(1)} %copy-done.6), kind=kOutput, calls=%fused_computation.70 | convolution fusion | flops 2883584 | bytes 2973952 | tf_op jit(solution)/shard_map/kgv,v->kg/dot_general | solution.py:43
  43.0 0.0 copy-start.8
  43.0 6.6 %copy.16 = f32[1,11264,2]{1,2,0:T(2,128)S(1)} copy(f32[1,11264,2]{0,1,2:T(8,128)} %fusion.48) | data formatting | bytes 180224 | tf_op jit(solution)/shard_map/kgv,v->kg/dot_general | solution.py:43
  49.6 0.2 fusion.17
  49.8 0.0 copy-done.3
  49.8 0.0 copy-done.8
  49.8 2.9 %fusion.43 = (f32[11264,2]{0,1:T(2,128)S(1)}, f32[11264,2,32]{0,2,1:T(8,128)}) fusion(bf16[11264,2,64]{0,2,1:T(8,128)(2,1)S(1)} %bitcast.69, f32[11264,2]{0,1:T(2,128)S(1)} %fusion.17, bf16[64,32]{0,1:T(8,128)(2,1)S(1)} %copy-done.8), kind=kOutput, calls=%fused_computation.67 | convolution fusion | flops 94437408 | bytes 5951488 | tf_op jit(solution)/shard_map/sub | solution.py:50
  52.7 0.0 copy-start.7
  52.7 2.3 %convert_reduce_fusion.1 = (f32[2,32]{1,0:T(2,128)S(1)}, bf16[11264,2,32]{0,2,1:T(8,128)(2,1)S(1)}) fusion(f32[11264,2,32]{0,2,1:T(8,128)} %get-tuple-element.10, f32[11264,2]{0,1:T(2,128)S(1)} %get-tuple-element.9), kind=kLoop, calls=%fused_computation.28 | loop fusion | flops 2883520 | bytes 4415744 | tf_op jit(solution)/shard_map/reduce_sum | solution.py:56
  55.1 2.7 %fusion.51 = f32[2,32,64]{2,1,0:T(8,128)S(1)} fusion(bf16[11264,2,32]{0,2,1:T(8,128)(2,1)S(1)} %get-tuple-element.8, bf16[11264,2,64]{0,2,1:T(8,128)(2,1)} %bitcast.70), kind=kOutput, calls=%fused_computation.72 | convolution fusion | flops 92274688 | bytes 4341760 | tf_op jit(solution)/shard_map/nhg,nhd->hgd/dot_general | solution.py:53
  57.7 25.9 %all-reduce = (f32[2,32,64]{2,1,0:T(8,128)S(1)}, f32[2,32]{1,0:T(2,128)S(1)}) all-reduce(f32[2,32,64]{2,1,0:T(8,128)S(1)} %fusion.51, f32[2,32]{1,0:T(2,128)S(1)} %get-tuple-element.7), channel_id=1, replica_groups=mesh['pts'=8,'wid'=4] {'pts'}, use_global_device_ids=true, to_apply=%region_4.5 | all-reduce | flops 4160 | bytes 33280 | tf_op jit(solution)/shard_map/psum | solution.py:57
  83.6 0.0 copy-done.7
  83.6 0.2 fusion.24
  83.8 0.2 fusion.26
  84.1 0.2 fusion.22
  84.3 0.2 fusion.44
  84.6 0.3 convolution_convert_fusion.2
  84.8 2.5 %fusion.2 = bf16[11264,2,64]{0,2,1:T(8,128)(2,1)} fusion(bf16[2,32,64]{2,1,0:T(8,128)(2,1)S(1)} %convolution_convert_fusion.2, bf16[11264,2,32]{0,2,1:T(8,128)(2,1)S(1)} %get-tuple-element.8), kind=kOutput, calls=%fused_computation.7 | convolution fusion | flops 93716480 | bytes 4333568 | tf_op jit(solution)/shard_map/nhg,hgd->nhd/dot_general | solution.py:68
  87.3 5.3 %all_to_all.14 = bf16[4,2816,128]{1,0,2:T(4,128)(2,1)S(1)} reshape(bf16[11264,2,64]{0,2,1:T(8,128)(2,1)} %fusion.2) | data formatting | bytes 5767168 | tf_op jit(solution)/shard_map/all_to_all | solution.py:72
  92.6 1.9 copy.13
  94.5 4.9 %all-to-all-start = ((bf16[4,2816,128]{1,2,0:T(8,128)(2,1)}), bf16[4,2816,128]{1,2,0:T(8,128)(2,1)S(1)}, u32[]{:S(2)}, u32[]{:S(2)}) async-start(bf16[4,2816,128]{1,2,0:T(8,128)(2,1)} %copy.13), calls=%async_computation | async-start | bytes 5767168 | tf_op jit(solution)/shard_map/all_to_all | solution.py:72
  99.4 0.0 copy-start.5
  99.4 13.0 %convert_element_type.33 = f32[11264,512]{0,1:T(8,128)} convert(bf16[11264,512]{0,1:T(8,128)(2,1)} %copy.12) | non-fusion elementwise | flops 5767168 | bytes 34603008 | tf_op jit(solution)/shard_map/convert_element_type | solution.py:37
  112.3 0.0 copy-done.5
  112.3 60.0 %all_gather.9 = bf16[512,512]{1,0:T(8,128)(2,1)S(1)} all-gather(bf16[128,512]{1,0:T(8,128)(2,1)S(1)} %copy-done.5), channel_id=1, replica_groups=mesh['pts'=8,'wid'=4] {'wid'}, dimensions={0}, use_global_device_ids=true | all-gather | bytes 655360 | tf_op jit(solution)/shard_map/all_gather | solution.py:74
  172.3 17.7 %all_gather.10 = bf16[512,512]{1,0:T(8,128)(2,1)} all-gather(bf16[128,512]{1,0:T(8,128)(2,1)} %param.14), channel_id=1, replica_groups=mesh['pts'=8,'wid'=4] {'wid'}, dimensions={0}, use_global_device_ids=true | all-gather | bytes 655360 | tf_op jit(solution)/shard_map/all_gather | solution.py:75
  190.1 16.3 %all_gather.11 = bf16[512,512]{1,0:T(8,128)(2,1)} all-gather(bf16[128,512]{1,0:T(8,128)(2,1)} %param.15), channel_id=1, replica_groups=mesh['pts'=8,'wid'=4] {'wid'}, dimensions={0}, use_global_device_ids=true | all-gather | bytes 655360 | tf_op jit(solution)/shard_map/all_gather | solution.py:76
  206.3 0.0 all-to-all-done
  206.3 4.4 %fusion.45 = (f32[2816]{0:T(1024)S(1)}, f32[2816,512]{0,1:T(8,128)S(1)}) fusion(bf16[2816,512]{0,1:T(8,128)(2,1)S(1)} %bitcast.67, bf16[512,512]{1,0:T(8,128)(2,1)S(1)} %all_gather.9, f32[11264,512]{0,1:T(8,128)} %convert_element_type.33, s32[]{:T(128)S(6)} %select_n.7), kind=kOutput, calls=%fused_computation.69 | convolution fusion | flops 1479275776 | bytes 14953476 | tf_op jit(solution)/shard_map/dot_general | solution.py:78
  210.7 0.0 copy-start.2
  210.7 0.0 copy-start.4
  210.7 2.4 %copy-done.2 = f32[2816,512]{0,1:T(8,128)} copy-done((f32[2816,512]{0,1:T(8,128)}, f32[2816,512]{0,1:T(8,128)S(1)}, u32[]{:S(2)}) %copy-start.2) | copy-done | bytes 5767192
  213.2 0.6 multiply_reduce_fusion.1
  213.8 0.6 add_rsqrt_fusion.1
  214.4 0.0 copy-done.4
  214.4 0.0 copy-start.1
  214.4 7.6 %add_convert_fusion = bf16[2816,512]{0,1:T(8,128)(2,1)S(1)} fusion(f32[2816,512]{0,1:T(8,128)} %copy-done.2, bf16[512,512]{1,0:T(8,128)(2,1)} %all_gather.11, bf16[512,512]{1,0:T(8,128)(2,1)S(1)} %copy-done.4, f32[2816]{0:T(1024)} %add_rsqrt_fusion.1, f32[2816]{0:T(1024)S(1)} %broadcast_multiply_fusion.1), kind=kOutput, calls=%fused_computation.21 | convolution fusion | flops 2972975104 | bytes 9721856 | tf_op jit(solution)/shard_map/dot_general | solution.py:85
  222.0 2.7 %copy.15 = bf16[2816,512]{1,0:T(8,128)(2,1)} copy(bf16[2816,512]{0,1:T(8,128)(2,1)S(1)} %add_convert_fusion) | data formatting | bytes 5767168 | tf_op jit(solution)/shard_map/convert_element_type | solution.py:85
  224.7 0.0 copy-done.1
  (5 shorter events, 0.1 us)
Async XLA Ops:
  0.0 29.5 %copy-start = (bf16[512,128]{1,0:T(8,128)(2,1)S(1)}, bf16[512,128]{1,0:T(8,128)(2,1)}, u32[]{:S(2)}) copy-start(bf16[512,128]{1,0:T(8,128)(2,1)} %param.9) | copy-start | bytes 393220
  29.5 8.1 %copy-start.6 = (f32[64]{0:T(128)S(1)}, f32[64]{0:T(128)}, u32[]{:S(2)}) copy-start(f32[64]{0:T(128)} %param.11) | copy-start | bytes 772
  37.6 12.2 %copy-start.3 = (bf16[11264,128]{0,1:T(8,128)(2,1)}, bf16[11264,128]{0,1:T(8,128)(2,1)S(1)}, u32[]{:S(2)}) copy-start(bf16[11264,128]{0,1:T(8,128)(2,1)S(1)} %convolution_convert_fusion.1) | copy-start | bytes 8650756
  43.0 6.8 %copy-start.8 = (bf16[64,32]{0,1:T(8,128)(2,1)S(1)}, bf16[64,32]{0,1:T(8,128)(2,1)}, u32[]{:S(2)}) copy-start(bf16[64,32]{0,1:T(8,128)(2,1)} %param.10) | copy-start | bytes 12292
  52.7 30.9 %copy-start.7 = (f32[3,64,64]{2,1,0:T(8,128)S(1)}, f32[3,64,64]{2,1,0:T(8,128)}, u32[]{:S(2)}) copy-start(f32[3,64,64]{2,1,0:T(8,128)} %param.12) | copy-start | bytes 147460
  94.5 111.9 %all-to-all-start = ((bf16[4,2816,128]{1,2,0:T(8,128)(2,1)}), bf16[4,2816,128]{1,2,0:T(8,128)(2,1)S(1)}, u32[]{:S(2)}, u32[]{:S(2)}) async-start(bf16[4,2816,128]{1,2,0:T(8,128)(2,1)} %copy.13), calls=%async_computation | async-start | bytes 5767168 | tf_op jit(solution)/shard_map/all_to_all | solution.py:72
  99.4 13.0 %copy-start.5 = (bf16[128,512]{1,0:T(8,128)(2,1)S(1)}, bf16[128,512]{1,0:T(8,128)(2,1)}, u32[]{:S(2)}) copy-start(bf16[128,512]{1,0:T(8,128)(2,1)} %param.13) | copy-start | bytes 393220
  210.7 2.5 %copy-start.2 = (f32[2816,512]{0,1:T(8,128)}, f32[2816,512]{0,1:T(8,128)S(1)}, u32[]{:S(2)}) copy-start(f32[2816,512]{0,1:T(8,128)S(1)} %get-tuple-element.14) | copy-start | bytes 17301508
  210.7 3.7 %copy-start.4 = (bf16[512,512]{1,0:T(8,128)(2,1)S(1)}, bf16[512,512]{1,0:T(8,128)(2,1)}, u32[]{:S(2)}) copy-start(bf16[512,512]{1,0:T(8,128)(2,1)} %all_gather.10) | copy-start | bytes 1572868
  214.4 10.3 %copy-start.1 = (bf16[512,128]{1,0:T(8,128)(2,1)S(1)}, bf16[512,128]{1,0:T(8,128)(2,1)}, u32[]{:S(2)}) copy-start(bf16[512,128]{1,0:T(8,128)(2,1)} %param.9) | copy-start | bytes 393220
where the time goes:
time: 226 us; the launch traced here: 225 us
  blocking collectives  120 us (53%)
  matrix products  34.7 us (15%)
  local copies, waits for them, and re-layouts  33.8 us (15%)
  other arithmetic  31.3 us (14%)
  starting transfers between devices  4.87 us (2%)
    all_gather x1, blocking collectives, local(): lax.all_gather(exit_matrix, 'wid', axis=0, tiled=True)  60 us
    psum x1, blocking collectives, local(): numerator, mass = lax.psum((numerator, mass), 'pts')  25.9 us
    all_gather x1, blocking collectives, local(): lax.all_gather(widening_matrix, 'wid', axis=0, tiled=True)  17.7 us
    unnamed x19, local copies, waits for them, and re-layouts  17.3 us
    all_gather x1, blocking collectives, local(): lax.all_gather(narrowing_matrix, 'wid', axis=0, tiled=True)  16.3 us
    convert_element_type x1, other arithmetic, local(): features = vertex_features.astype(jnp.float32)  13 us
    dot_general x1, matrix products, local(): jnp.dot(normed, entry_matrix, preferred_element_type=jnp.float32)  8.08 us
    reduce_sum x2, other arithmetic, layer_norm(): variance = jnp.mean(centred * centred, axis=-1, keepdims=True)  8.01 us
  transfers between devices with their start and end apart: 1, of which 0 were waited for; matrix products, arithmetic and copies ran while one was open for 6% of the time, Pallas kernels for 0%

commit v1 on v0

--- a/solution.py
+++ b/solution.py
@@ -69,7 +69,9 @@
         "nhg,hgd->nhd", partition_mapping, out_tok, preferred_element_type=jnp.float32
     ).astype(jnp.bfloat16)
     deslice = deslice.reshape(point_rows, local_heads * head_size)
-    mixed_rows = lax.all_to_all(deslice, "wid", split_axis=0, concat_axis=1, tiled=True)
+    pieces = jnp.split(deslice, lax.axis_size("wid"), axis=0)
+    arrived = lax.all_to_all(jnp.stack(pieces), "wid", 0, 0)
+    mixed_rows = jnp.concatenate(arrived, axis=1)
     out_full, up_full, down_full = (
         lax.all_gather(exit_matrix, "wid", axis=0, tiled=True),
         lax.all_gather(widening_matrix, "wid", axis=0, tiled=True),

time: 226 us -> 219 us (0.969)
  local copies, waits for them, and re-layouts: 33.8 us -> 26.9 us
    all_to_all x2 -> x0, local copies, waits for them, and re-layouts: 7.14 us -> none  [local(): lax.all_to_all(deslice, 'wid', split_axis=0, concat_axis=1, tiled=True)]
where the time goes in v1:
time: 219 us; the launch traced here: 218 us
  blocking collectives  120 us (55%)
  other arithmetic  33.1 us (15%)
  matrix products  33.1 us (15%)
  local copies, waits for them, and re-layouts  26.9 us (12%)
  starting transfers between devices  4.87 us (2%)
    all_gather x1, blocking collectives, local(): lax.all_gather(exit_matrix, 'wid', axis=0, tiled=True)  60 us
    psum x1, blocking collectives, local(): numerator, mass = lax.psum((numerator, mass), 'pts')  25.9 us
    all_gather x1, blocking collectives, local(): lax.all_gather(widening_matrix, 'wid', axis=0, tiled=True)  17.7 us
    unnamed x19, local copies, waits for them, and re-layouts  17.3 us
    all_gather x1, blocking collectives, local(): lax.all_gather(narrowing_matrix, 'wid', axis=0, tiled=True)  16.3 us
    convert_element_type x1, other arithmetic, local(): features = vertex_features.astype(jnp.float32)  13 us
    dot_general x1, matrix products, local(): jnp.dot(normed, entry_matrix, preferred_element_type=jnp.float32)  8.08 us
    reduce_sum x2, other arithmetic, layer_norm(): variance = jnp.mean(centred * centred, axis=-1, keepdims=True)  8.01 us
  transfers between devices with their start and end apart: 1, of which 0 were waited for; matrix products, arithmetic and copies ran while one was open for 6% of the time, Pallas kernels for 0%

profile of v1, /device:TPU:0, one launch (start us, length us, event | category | flops | bytes accessed | tf_op | source)
XLA Modules:
  0.0 218.0 jit_solution(1795988380376830576)
XLA Ops:
  0.0 0.0 copy-start
  0.0 14.9 %copy.9 = bf16[11264,512]{0,1:T(8,128)(2,1)} copy(bf16[11264,512]{1,0:T(8,128)(2,1)} %param.8) | data formatting | bytes 23068672 | tf_op args[0]
  14.9 7.2 %convert_reduce_fusion = f32[11264]{0:T(1024)S(1)} fusion(bf16[11264,512]{0,1:T(8,128)(2,1)} %copy.9), kind=kLoop, calls=%fused_computation.3 | loop fusion | flops 11523072 | bytes 11579392 | tf_op jit(solution)/shard_map/reduce_sum | solution.py:8
  22.0 7.4 %multiply_reduce_fusion = f32[11264]{0:T(1024)S(1)} fusion(bf16[11264,512]{0,1:T(8,128)(2,1)} %copy.9, f32[11264]{0:T(1024)S(1)} %broadcast_multiply_fusion), kind=kLoop, calls=%fused_computation.2 | loop fusion | flops 23057408 | bytes 11624448 | tf_op jit(solution)/shard_map/reduce_sum | solution.py:9
  29.5 0.0 copy-done
  29.5 0.0 copy-start.6
  29.5 8.1 %convolution_convert_fusion.1 = bf16[11264,128]{0,1:T(8,128)(2,1)S(1)} fusion(bf16[512,128]{1,0:T(8,128)(2,1)S(1)} %copy-done, bf16[11264,512]{0,1:T(8,128)(2,1)} %copy.9, f32[11264]{0:T(1024)S(1)} %add_rsqrt_fusion, f32[11264]{0:T(1024)S(1)} %broadcast_multiply_fusion), kind=kOutput, calls=%fused_computation.5 | convolution fusion | flops 1500905472 | bytes 14639104 | tf_op jit(solution)/shard_map/dot_general | solution.py:39
  37.6 0.0 copy-start.3
  37.6 0.0 copy-done.6
  37.6 5.4 %fusion.49 = f32[1,11264,2]{0,1,2:T(8,128)} fusion(bf16[11264,2,64]{0,2,1:T(8,128)(2,1)S(1)} %bitcast.70, f32[64]{0:T(128)S(1)} %copy-done.6), kind=kOutput, calls=%fused_computation.72 | convolution fusion | flops 2883584 | bytes 2973952 | tf_op jit(solution)/shard_map/kgv,v->kg/dot_general | solution.py:43
  43.0 0.0 copy-start.8
  43.0 6.6 %copy.12 = f32[1,11264,2]{1,2,0:T(2,128)S(1)} copy(f32[1,11264,2]{0,1,2:T(8,128)} %fusion.49) | data formatting | bytes 180224 | tf_op jit(solution)/shard_map/kgv,v->kg/dot_general | solution.py:43
  49.6 0.2 fusion.17
  49.8 0.0 copy-done.3
  49.8 0.0 copy-done.8
  49.8 2.9 %fusion.44 = (f32[11264,2]{0,1:T(2,128)S(1)}, f32[11264,2,32]{0,2,1:T(8,128)}) fusion(bf16[11264,2,64]{0,2,1:T(8,128)(2,1)S(1)} %bitcast.71, f32[11264,2]{0,1:T(2,128)S(1)} %fusion.17, bf16[64,32]{0,1:T(8,128)(2,1)S(1)} %copy-done.8), kind=kOutput, calls=%fused_computation.69 | convolution fusion | flops 94437408 | bytes 5951488 | tf_op jit(solution)/shard_map/sub | solution.py:50
  52.7 0.0 copy-start.7
  52.7 2.3 %convert_reduce_fusion.1 = (f32[2,32]{1,0:T(2,128)S(1)}, bf16[11264,2,32]{0,2,1:T(8,128)(2,1)S(1)}) fusion(f32[11264,2,32]{0,2,1:T(8,128)} %get-tuple-element.14, f32[11264,2]{0,1:T(2,128)S(1)} %get-tuple-element.13), kind=kLoop, calls=%fused_computation.29 | loop fusion | flops 2883520 | bytes 4415744 | tf_op jit(solution)/shard_map/reduce_sum | solution.py:56
  55.1 2.7 %fusion.52 = f32[2,32,64]{2,1,0:T(8,128)S(1)} fusion(bf16[11264,2,32]{0,2,1:T(8,128)(2,1)S(1)} %get-tuple-element.8, bf16[11264,2,64]{0,2,1:T(8,128)(2,1)} %bitcast.72), kind=kOutput, calls=%fused_computation.74 | convolution fusion | flops 92274688 | bytes 4341760 | tf_op jit(solution)/shard_map/nhg,nhd->hgd/dot_general | solution.py:53
  57.7 25.9 %all-reduce = (f32[2,32,64]{2,1,0:T(8,128)S(1)}, f32[2,32]{1,0:T(2,128)S(1)}) all-reduce(f32[2,32,64]{2,1,0:T(8,128)S(1)} %fusion.52, f32[2,32]{1,0:T(2,128)S(1)} %get-tuple-element.7), channel_id=1, replica_groups=mesh['pts'=8,'wid'=4] {'pts'}, use_global_device_ids=true, to_apply=%region_4.5 | all-reduce | flops 4160 | bytes 33280 | tf_op jit(solution)/shard_map/psum | solution.py:57
  83.6 0.0 copy-done.7
  83.6 0.2 fusion.24
  83.8 0.2 fusion.26
  84.1 0.2 fusion.22
  84.3 0.2 fusion.45
  84.6 0.3 convolution_convert_fusion.2
  84.8 0.9 fusion.2
  85.8 0.2 fusion.43
  86.0 1.8 pad_maximum_fusion
  87.8 4.9 %all-to-all-start = ((bf16[4,2816,128]{1,2,0:T(8,128)(2,1)}), bf16[4,2816,128]{1,2,0:T(8,128)(2,1)S(1)}, u32[]{:S(2)}, u32[]{:S(2)}) async-start(bf16[4,2816,128]{1,2,0:T(8,128)(2,1)} %pad_maximum_fusion), calls=%async_computation | async-start | bytes 5767168 | tf_op jit(solution)/shard_map/all_to_all | solution.py:73
  92.6 0.0 copy-start.5
  92.6 13.0 %convert_element_type.33 = f32[11264,512]{0,1:T(8,128)} convert(bf16[11264,512]{0,1:T(8,128)(2,1)} %copy.9) | non-fusion elementwise | flops 5767168 | bytes 34603008 | tf_op jit(solution)/shard_map/convert_element_type | solution.py:37
  105.6 0.0 copy-done.5
  105.6 60.0 %all_gather.9 = bf16[512,512]{1,0:T(8,128)(2,1)S(1)} all-gather(bf16[128,512]{1,0:T(8,128)(2,1)S(1)} %copy-done.5), channel_id=1, replica_groups=mesh['pts'=8,'wid'=4] {'wid'}, dimensions={0}, use_global_device_ids=true | all-gather | bytes 655360 | tf_op jit(solution)/shard_map/all_gather | solution.py:76
  165.6 17.7 %all_gather.10 = bf16[512,512]{1,0:T(8,128)(2,1)} all-gather(bf16[128,512]{1,0:T(8,128)(2,1)} %param.14), channel_id=1, replica_groups=mesh['pts'=8,'wid'=4] {'wid'}, dimensions={0}, use_global_device_ids=true | all-gather | bytes 655360 | tf_op jit(solution)/shard_map/all_gather | solution.py:77
  183.3 16.3 %all_gather.11 = bf16[512,512]{1,0:T(8,128)(2,1)} all-gather(bf16[128,512]{1,0:T(8,128)(2,1)} %param.15), channel_id=1, replica_groups=mesh['pts'=8,'wid'=4] {'wid'}, dimensions={0}, use_global_device_ids=true | all-gather | bytes 655360 | tf_op jit(solution)/shard_map/all_gather | solution.py:78
  199.6 0.0 all-to-all-done
  199.6 4.4 %fusion.46 = (f32[2816]{0:T(1024)S(1)}, f32[2816,512]{0,1:T(8,128)S(1)}) fusion(bf16[2816,512]{0,1:T(8,128)(2,1)S(1)} %bitcast.69, bf16[512,512]{1,0:T(8,128)(2,1)S(1)} %all_gather.9, f32[11264,512]{0,1:T(8,128)} %convert_element_type.33, s32[]{:T(128)S(6)} %select_n.7), kind=kOutput, calls=%fused_computation.71 | convolution fusion | flops 1479275776 | bytes 14953476 | tf_op jit(solution)/shard_map/dot_general | solution.py:80
  204.0 0.0 copy-start.2
  204.0 0.0 copy-start.4
  204.0 2.4 %copy-done.2 = f32[2816,512]{0,1:T(8,128)} copy-done((f32[2816,512]{0,1:T(8,128)}, f32[2816,512]{0,1:T(8,128)S(1)}, u32[]{:S(2)}) %copy-start.2) | copy-done | bytes 5767192
  206.5 0.6 multiply_reduce_fusion.1
  207.1 0.6 add_rsqrt_fusion.1
  207.7 0.0 copy-done.4
  207.7 0.0 copy-start.1
  207.7 7.6 %add_convert_fusion = bf16[2816,512]{0,1:T(8,128)(2,1)S(1)} fusion(f32[2816,512]{0,1:T(8,128)} %copy-done.2, bf16[512,512]{1,0:T(8,128)(2,1)} %all_gather.11, bf16[512,512]{1,0:T(8,128)(2,1)S(1)} %copy-done.4, f32[2816]{0:T(1024)} %add_rsqrt_fusion.1, f32[2816]{0:T(1024)S(1)} %broadcast_multiply_fusion.1), kind=kOutput, calls=%fused_computation.21 | convolution fusion | flops 2972975104 | bytes 9721856 | tf_op jit(solution)/shard_map/dot_general | solution.py:87
  215.3 2.7 %copy.11 = bf16[2816,512]{1,0:T(8,128)(2,1)} copy(bf16[2816,512]{0,1:T(8,128)(2,1)S(1)} %add_convert_fusion) | data formatting | bytes 5767168 | tf_op jit(solution)/shard_map/convert_element_type | solution.py:87
  218.0 0.0 copy-done.1
  (5 shorter events, 0.1 us)
Async XLA Ops:
  0.0 29.5 %copy-start = (bf16[512,128]{1,0:T(8,128)(2,1)S(1)}, bf16[512,128]{1,0:T(8,128)(2,1)}, u32[]{:S(2)}) copy-start(bf16[512,128]{1,0:T(8,128)(2,1)} %param.9) | copy-start | bytes 393220
  29.5 8.1 %copy-start.6 = (f32[64]{0:T(128)S(1)}, f32[64]{0:T(128)}, u32[]{:S(2)}) copy-start(f32[64]{0:T(128)} %param.11) | copy-start | bytes 772
  37.6 12.2 %copy-start.3 = (bf16[11264,128]{0,1:T(8,128)(2,1)}, bf16[11264,128]{0,1:T(8,128)(2,1)S(1)}, u32[]{:S(2)}) copy-start(bf16[11264,128]{0,1:T(8,128)(2,1)S(1)} %convolution_convert_fusion.1) | copy-start | bytes 8650756
  43.0 6.8 %copy-start.8 = (bf16[64,32]{0,1:T(8,128)(2,1)S(1)}, bf16[64,32]{0,1:T(8,128)(2,1)}, u32[]{:S(2)}) copy-start(bf16[64,32]{0,1:T(8,128)(2,1)} %param.10) | copy-start | bytes 12292
  52.7 30.9 %copy-start.7 = (f32[3,64,64]{2,1,0:T(8,128)S(1)}, f32[3,64,64]{2,1,0:T(8,128)}, u32[]{:S(2)}) copy-start(f32[3,64,64]{2,1,0:T(8,128)} %param.12) | copy-start | bytes 147460
  87.8 111.9 %all-to-all-start = ((bf16[4,2816,128]{1,2,0:T(8,128)(2,1)}), bf16[4,2816,128]{1,2,0:T(8,128)(2,1)S(1)}, u32[]{:S(2)}, u32[]{:S(2)}) async-start(bf16[4,2816,128]{1,2,0:T(8,128)(2,1)} %pad_maximum_fusion), calls=%async_computation | async-start | bytes 5767168 | tf_op jit(solution)/shard_map/all_to_all | solution.py:73
  92.6 13.0 %copy-start.5 = (bf16[128,512]{1,0:T(8,128)(2,1)S(1)}, bf16[128,512]{1,0:T(8,128)(2,1)}, u32[]{:S(2)}) copy-start(bf16[128,512]{1,0:T(8,128)(2,1)} %param.13) | copy-start | bytes 393220
  204.0 2.5 %copy-start.2 = (f32[2816,512]{0,1:T(8,128)}, f32[2816,512]{0,1:T(8,128)S(1)}, u32[]{:S(2)}) copy-start(f32[2816,512]{0,1:T(8,128)S(1)} %get-tuple-element.18) | copy-start | bytes 17301508
  204.0 3.7 %copy-start.4 = (bf16[512,512]{1,0:T(8,128)(2,1)S(1)}, bf16[512,512]{1,0:T(8,128)(2,1)}, u32[]{:S(2)}) copy-start(bf16[512,512]{1,0:T(8,128)(2,1)} %all_gather.10) | copy-start | bytes 1572868
  207.7 10.3 %copy-start.1 = (bf16[512,128]{1,0:T(8,128)(2,1)S(1)}, bf16[512,128]{1,0:T(8,128)(2,1)}, u32[]{:S(2)}) copy-start(bf16[512,128]{1,0:T(8,128)(2,1)} %param.9) | copy-start | bytes 393220
